TPU v7x, 8 devices: a whole 2x2x1 slice. The times are simulated.
8 devices in a mesh: rep: 1 (over z), pp: 8 (over x, y, core).
Axes of the slice: x: 2, y: 2, z: 1, core: 2. Of those that a mesh axis runs over, the one named last changes fastest.
Arguments:
- x: bfloat16 [16, 512, 512], P('rep')
- dy: bfloat16 [16, 512, 512], P('rep')
- w_gate: bfloat16 [8, 512, 1536], P('pp')
- w_up: bfloat16 [8, 512, 1536], P('pp')
- w_down: bfloat16 [8, 1536, 512], P('pp')
Outputs:
- output 1: bfloat16 [8, 512, 1536], P(('rep', 'pp'))
- output 2: bfloat16 [8, 512, 1536], P(('rep', 'pp'))
- output 3: bfloat16 [8, 1536, 512], P(('rep', 'pp'))
All inputs are finite; a program needn't handle non-finite values.
Results may differ from a plain program's by a relative error of at most 0.0277.
Values are sent between devices in bfloat16 or wider.
A program may use at most 2 GiB of HBM per device.

v0:
```python
import jax
import jax.numpy as jnp
from jax import lax
from jax.sharding import PartitionSpec as P

NAMES = ("w_gate", "w_up", "w_down")


def matmul(a, w):
    return jnp.dot(a, w, preferred_element_type=jnp.float32).astype(jnp.bfloat16)


def normed(h):
    wide = h.astype(jnp.float32)
    scale = lax.rsqrt(jnp.mean(wide**2, -1, keepdims=True) + 1e-6)
    return (wide * scale).astype(jnp.bfloat16)


def layer(h, w):
    a = normed(h)
    gate = jnp.dot(a, w["w_gate"], preferred_element_type=jnp.float32)
    up = jnp.dot(a, w["w_up"], preferred_element_type=jnp.float32)
    return h + matmul((jax.nn.silu(gate) * up).astype(jnp.bfloat16), w["w_down"])


def stage(weights, h):
    for number in range(weights["w_gate"].shape[0]):
        h = layer(h, {name: w[number] for name, w in weights.items()})
    return h


def solution(mesh):
    stages = mesh.shape["pp"]
    onward = [(i, i + 1) for i in range(stages - 1)]
    back_again = [(i + 1, i) for i in range(stages - 1)]

    def step(x, dy, *arrays):
        weights = dict(zip(NAMES, arrays, strict=True))
        micro, me = x.shape[0], lax.axis_index("pp")
        kept, came = jnp.zeros_like(x), jnp.zeros_like(x[0])
        for t in range(micro + stages - 1):
            number = jnp.clip(t - me, 0, micro - 1)
            at_work = (t >= me) & (t - me < micro)
            h = jnp.where(me == 0, x[min(t, micro - 1)], came)
            was = lax.dynamic_index_in_dim(kept, number, 0, keepdims=False)
            kept = lax.dynamic_update_index_in_dim(kept, jnp.where(at_work, h, was), number, 0)
            came = lax.ppermute(stage(weights, h), "pp", onward)
        total = {name: jnp.zeros(w.shape, jnp.float32) for name, w in weights.items()}
        came, behind = jnp.zeros_like(x[0]), stages - 1 - me
        for t in range(micro + stages - 1):
            number = jnp.clip(t - behind, 0, micro - 1)
            at_work = (t >= behind) & (t - behind < micro)
            by_y = jnp.where(behind == 0, dy[min(t, micro - 1)], came)
            _, back = jax.vjp(stage, weights, lax.dynamic_index_in_dim(kept, number, 0, keepdims=False))
            by_w, by_h = back(by_y)
            total = {name: total[name] + jnp.where(at_work, by_w[name].astype(jnp.float32), 0.0) for name in NAMES}
            came = lax.ppermute(by_h, "pp", back_again)
        return tuple(total[name].astype(jnp.bfloat16) for name in NAMES)

    return jax.shard_map(
        step,
        mesh=mesh,
        in_specs=(P("rep", None, None),) * 2 + (P("pp", None, None),) * 3,
        out_specs=(P(("rep", "pp"), None, None),) * 3,
        check_vma=False,
    )
```

profile of v0, /device:TPU:5, one launch (start us, length us, event | category | flops | bytes accessed | tf_op | source)
XLA Modules:
  0.0 1178.3 jit_solution(14073269648924388293)
XLA Ops:
  15.0 6.1 collective-permute-done
  25.8 5.7 fusion.831
  36.9 6.1 collective-permute-done.1
  47.7 5.7 fusion.828
  58.8 6.1 collective-permute-done.2
  69.7 5.7 fusion.825
  80.9 5.9 collective-permute-done.3
  91.6 5.7 fusion.822
  102.6 6.1 collective-permute-done.4
  113.5 5.7 fusion.819
  124.6 6.1 collective-permute-done.5
  135.4 5.7 fusion.816
  146.5 6.1 collective-permute-done.6
  157.3 5.7 fusion.813
  168.6 5.9 collective-permute-done.7
  179.3 5.7 fusion.810
  190.3 6.1 collective-permute-done.8
  201.3 5.8 fusion.807
  212.4 6.0 collective-permute-done.9
  619.4 6.8 collective-permute-done.24
  1112.3 5.9 collective-permute-done.43
  1124.5 17.4 %fusion.102 = bf16[1,512,1536]{2,1,0:T(8,128)(2,1)} fusion(bf16[512,1536]{1,0:T(8,128)(2,1)} %copy-done.105, bf16[512,1536]{1,0:T(8,128)(2,1)} %convolution_convert_fusion.46, bf16[512,1536]{1,0:T(8,128)(2,1)} %convolution_convert_fusion.47, bf16[512,1536]{1,0:T(8,128)(2,1)} %convolution_convert_fusion.48, ...), kind=kOutput, calls=%fused_computation.329 | convolution fusion | flops 865861632 | bytes 41420828 | tf_op jit(solution)/shard_map/transpose(jvp())/dot_general | solution.py:22
  1141.9 18.2 %fusion.101 = bf16[1,512,1536]{2,1,0:T(8,128)(2,1)} fusion(bf16[512,1536]{1,0:T(8,128)(2,1)} %fusion.74, bf16[512,1536]{1,0:T(8,128)(2,1)S(1)} %copy-done.108, bf16[512,1536]{1,0:T(8,128)(2,1)} %convolution_convert_fusion.69, bf16[512,1536]{1,0:T(8,128)(2,1)} %convolution_convert_fusion.70, bf16[512,1536]{1,0:T(8,128)(2,1)} %convolution_convert_fusion.71, ...), kind=kOutput, calls=%fused_computation.328 | convolution fusion | flops 860356608 | bytes 38275100 | tf_op jit(solution)/shard_map/transpose(jvp())/dot_general | solution.py:21
  1160.1 17.9 %fusion.100 = bf16[1,1536,512]{2,1,0:T(8,128)(2,1)} fusion(bf16[1536,512]{1,0:T(8,128)(2,1)} %convolution_convert_fusion.1, bf16[1536,512]{1,0:T(8,128)(2,1)} %convolution_convert_fusion.2, bf16[1536,512]{1,0:T(8,128)(2,1)} %convolution_convert_fusion.3, bf16[1536,512]{1,0:T(8,128)(2,1)} %convolution_convert_fusion.4, ...), kind=kOutput, calls=%fused_computation.327 | convolution fusion | flops 865337344 | bytes 43515928 | tf_op jit(solution)/shard_map/transpose(jvp())/dot_general | solution.py:10
  (692 shorter events, 996.2 us)
Async XLA Ops:
  228.7 14.7 %collective-permute-start.10 = (bf16[512,512]{1,0:T(8,128)(2,1)}, bf16[512,512]{1,0:T(8,128)(2,1)S(1)}, u32[]{:S(2)}, u32[]{:S(2)}) collective-permute-start(bf16[512,512]{1,0:T(8,128)(2,1)} %fusion.804), channel_id=1, source_target_pairs={{0,1},{1,2},{2,3},{3,4},{4,5},{5,6},{6,7}} | collective-permute-start | bytes 1572872 | tf_op jit(solution)/shard_map/ppermute | solution.py:47
  272.1 12.2 %collective-permute-start.12 = (bf16[512,512]{1,0:T(8,128)(2,1)}, bf16[512,512]{1,0:T(8,128)(2,1)S(1)}, u32[]{:S(2)}, u32[]{:S(2)}) collective-permute-start(bf16[512,512]{1,0:T(8,128)(2,1)} %fusion.798), channel_id=1, source_target_pairs={{0,1},{1,2},{2,3},{3,4},{4,5},{5,6},{6,7}} | collective-permute-start | bytes 1572872 | tf_op jit(solution)/shard_map/ppermute | solution.py:47
  294.5 11.5 collective-permute-start.13
  316.2 11.4 collective-permute-start.14
  337.8 11.5 collective-permute-start.15
  402.6 11.4 collective-permute-start.18
  424.2 11.8 collective-permute-start.19
  502.9 66.3 %collective-permute-start.22 = (bf16[512,512]{1,0:T(8,128)(2,1)S(1)}, bf16[512,512]{1,0:T(8,128)(2,1)S(1)}, u32[]{:S(2)}, u32[]{:S(2)}) collective-permute-start(bf16[512,512]{1,0:T(8,128)(2,1)S(1)} %fusion.1105), channel_id=1, source_target_pairs={{1,0},{2,1},{3,2},{4,3},{5,4},{6,5},{7,6}} | collective-permute-start | bytes 1572872 | tf_op jit(solution)/shard_map/ppermute | solution.py:57
  585.0 14.2 %collective-permute-start.23 = (bf16[512,512]{1,0:T(8,128)(2,1)S(1)}, bf16[512,512]{1,0:T(8,128)(2,1)S(1)}, u32[]{:S(2)}, u32[]{:S(2)}) collective-permute-start(bf16[512,512]{1,0:T(8,128)(2,1)S(1)} %fusion.1104), channel_id=1, source_target_pairs={{1,0},{2,1},{3,2},{4,3},{5,4},{6,5},{7,6}} | collective-permute-start | bytes 1572872 | tf_op jit(solution)/shard_map/ppermute | solution.py:57
  613.7 12.6 %collective-permute-start.24 = (bf16[512,512]{1,0:T(8,128)(2,1)S(1)}, bf16[512,512]{1,0:T(8,128)(2,1)S(1)}, u32[]{:S(2)}, u32[]{:S(2)}) collective-permute-start(bf16[512,512]{1,0:T(8,128)(2,1)S(1)} %fusion.1103), channel_id=1, source_target_pairs={{1,0},{2,1},{3,2},{4,3},{5,4},{6,5},{7,6}} | collective-permute-start | bytes 1572872 | tf_op jit(solution)/shard_map/ppermute | solution.py:57
  640.7 11.4 collective-permute-start.25
  666.6 11.4 collective-permute-start.26
  692.4 11.4 collective-permute-start.27
  718.2 11.4 collective-permute-start.28
  744.1 11.4 collective-permute-start.29
  769.9 11.4 collective-permute-start.30
  795.7 11.4 collective-permute-start.31
  821.5 11.4 collective-permute-start.32
  847.3 11.4 collective-permute-start.33
  898.9 11.4 collective-permute-start.35
  924.7 11.4 collective-permute-start.36
  1002.2 11.4 collective-permute-start.39
  1028.0 11.4 collective-permute-start.40
  1079.8 11.4 collective-permute-start.42
  (131 other events, 1183.7 us)
where the time goes:
time: 1200 us; the launch traced here: 1180 us
  matrix products  684 us (57%)
  waiting for transfers between devices  176 us (15%)
  starting transfers between devices  153 us (13%)
  other arithmetic  107 us (9%)
  local copies, waits for them, and re-layouts  53.9 us (4%)
    dot_general x90, matrix products, layer(): gate = jnp.dot(a, w['w_gate'], preferred_element_type=jnp.float32)  241 us
    dot_general x68, matrix products, layer(): up = jnp.dot(a, w['w_up'], preferred_element_type=jnp.float32)  227 us
    dot_general x68, matrix products, matmul(): jnp.dot(a, w, preferred_element_type=jnp.float32).astype(jnp.bfloat16)  216 us
    ppermute x22, waiting for transfers between devices, step(): came = lax.ppermute(by_h, 'pp', back_again)  113 us
    ppermute x22, starting transfers between devices, step(): came = lax.ppermute(stage(weights, h), 'pp', onward)  105 us
    ppermute x22, waiting for transfers between devices, step(): came = lax.ppermute(stage(weights, h), 'pp', onward)  62.9 us
    ppermute x22, starting transfers between devices, step(): came = lax.ppermute(by_h, 'pp', back_again)  48 us
    dynamic_update_slice x23, other arithmetic, step(): lax.dynamic_update_index_in_dim(kept, jnp.where(at_work, h, was), number, 0)  44 us
  transfers between devices with their start and end apart: 44, of which 32 were waited for; matrix products, arithmetic and copies ran while one was open for 19% of the time, Pallas kernels for 0%

commit v1 on v0

v1 whole, which is shorter than its diff:
```python
import functools

import jax
import jax.numpy as jnp
from jax import lax
from jax.experimental import pallas as pl
from jax.experimental.pallas import tpu as pltpu
from jax.sharding import PartitionSpec as P

f32, bf16 = jnp.float32, jnp.bfloat16
SLOTS = 3
OUTS = 4
PIECES = 4
FILL = 2
DRAIN = 2
TILE = 256


def dot(a, b):
    return jnp.dot(a, b, preferred_element_type=f32)


def dot_t(a, b):
    return lax.dot_general(a, b, (((1,), (1,)), ((), ())), preferred_element_type=f32)


def normed(h):
    wide = h.astype(f32)
    scale = lax.rsqrt(jnp.mean(wide * wide, -1, keepdims=True) + 1e-6)
    return wide, scale


def forward(h_ref, wg, wu, wd, si_ref, m_ref, hid_ref, out_ref):
    wide, scale = normed(h_ref[...])
    a = (wide * scale).astype(bf16)
    for j in range(wg.shape[1] // TILE):
        cs = pl.ds(j * TILE, TILE)
        g, u = dot(a, wg[:, cs]), dot(a, wu[:, cs])
        s = 1.0 / (1.0 + jnp.exp(-g))
        si = g * s
        si_ref[:, cs] = si
        m_ref[:, cs] = u * (s + si * (1.0 - s))
        hid_ref[:, cs] = (si * u).astype(bf16)
    if out_ref is not None:
        for j in range(wd.shape[1] // TILE):
            cs = pl.ds(j * TILE, TILE)
            out_ref[:, cs] = h_ref[:, cs] + dot(hid_ref[...], wd[:, cs]).astype(bf16)


def backward(h_ref, dy_ref, wg, wu, wd, si_ref, m_ref, dg_ref, du_ref, at_ref, gt_ref, through):
    dy = dy_ref[...]
    for j in range(wg.shape[1] // TILE):
        cs = pl.ds(j * TILE, TILE)
        dh = dot_t(dy, wd[cs, :]).astype(bf16).astype(f32)
        dg_ref[:, cs] = (dh * m_ref[:, cs]).astype(bf16)
        du_ref[:, cs] = (dh * si_ref[:, cs]).astype(bf16)
    wide, scale = normed(h_ref[...])
    at_ref[...] = (wide * scale).astype(bf16).T
    gt_ref[...] = dy.T
    if through:
        da = dot_t(dg_ref[...], wg[...]).astype(bf16) + dot_t(du_ref[...], wu[...]).astype(bf16)
        da = da.astype(f32)
        c = jnp.mean(da * wide, -1, keepdims=True) * (scale * scale)
        dy_ref[...] = dy + (scale * (da - wide * c)).astype(bf16)


def weights_term(acc, left, right):
    for j in range(right.shape[1] // TILE):
        cs = pl.ds(j * TILE, TILE)
        acc[:, cs] += dot(left[...], right[:, cs]).astype(bf16).astype(f32)


def kernel(stages, x, dy, wg_h, wu_h, wd_h, og, ou, od, si_h, m_h, hid_h,
           wg, wu, wd, acc_g, acc_u, acc_d, h_v, g_v, h_out, si_v, m_v, hid_v, dg_v, du_v, at_v, gt_v,
           w_sem, h_sem, g_sem, hs_sem, gs_sem, out_sem, in_sem, o_sem):
    me = lax.axis_index("pp")
    micro, rows = x.shape[0], x.shape[1]
    first, last = me == 0, me == stages - 1
    ahead = jnp.where(me >= stages - SLOTS, stages - me, 2 * (stages - me) - 2)
    ahead = jnp.minimum(ahead, 12)
    spill = me < stages - SLOTS

    barrier = pltpu.get_barrier_semaphore()

    for peer in range(stages - 1):
        to = lax.rem(me + peer + 1, stages)
        pl.semaphore_signal(barrier, inc=1, device_id={"pp": to}, device_id_type=pl.DeviceIdType.MESH)

    loads = [pltpu.make_async_copy(a.at[0], b, w_sem.at[i]) for i, (a, b) in enumerate(((wg_h, wg), (wu_h, wu), (wd_h, wd)))]

    def pieces(m, count, to, sem):
        size = rows // count
        for p in range(count):
            at = pl.ds(p * size, size)
            pltpu.make_async_copy(to[0].at[m, at], to[1].at[m, at], sem.at[m, p]).start()

    @pl.when(first)
    def _():
        pieces(0, FILL, (x, h_v), h_sem)

    for load in loads:
        load.start()

    @pl.when(first)
    def _():
        @pl.loop(1, micro)
        def _(m):
            pieces(m, 1, (x, h_v), h_sem)

    @pl.when(last)
    def _():
        pieces(micro - 1, DRAIN, (dy, g_v), g_sem)

        @pl.loop(0, micro - 1)
        def _(m):
            pieces(m, 1, (dy, g_v), g_sem)

    for acc in (acc_g, acc_u, acc_d):
        acc[...] = jnp.zeros_like(acc)
    for load in loads:
        load.wait()

    pl.semaphore_wait(barrier, stages - 1)

    def arrived(buf, sem, m, p, at):
        pltpu.make_async_copy(buf.at[m, at], buf.at[m, at], sem.at[m, p]).wait()

    def send_h(m, p, at):
        o = lax.rem(m, OUTS)
        return pltpu.make_async_remote_copy(
            h_out.at[o, at], h_v.at[m, at], hs_sem.at[o], h_sem.at[m, p], device_id={"pp": me + 1}, device_id_type=pl.DeviceIdType.MESH
        )

    def send_g(m, p, at):
        return pltpu.make_async_remote_copy(
            g_v.at[m, at], g_v.at[m, at], gs_sem.at[m], g_sem.at[m, p], device_id={"pp": me - 1}, device_id_type=pl.DeviceIdType.MESH
        )

    whole = pl.ds(0, rows)
    saved = ((si_v, si_h), (m_v, m_h), (hid_v, hid_h))

    def spill_out(m):
        return [pltpu.make_async_copy(v.at[0], h.at[m], out_sem.at[i]) for i, (v, h) in enumerate(saved)]

    def spill_in(m):
        slot = 1 + lax.rem(m, 2)
        return [pltpu.make_async_copy(h.at[m], v.at[slot], in_sem.at[lax.rem(m, 2), i]) for i, (v, h) in enumerate(saved)]

    def do_forward(m):
        slot = jnp.where(spill, 0, lax.rem(m, SLOTS))

        @pl.when(spill & (m > 0))
        def _():
            for copy in spill_out(m - 1):
                copy.wait()

        @pl.when((m >= OUTS) & (me < stages - 1))
        def _():
            send_h(m - OUTS, 0, whole).wait_send()

        def piece(p, count, out):
            size = rows // count
            at = pl.ds(pl.multiple_of(p * size, size), size)
            arrived(h_v, h_sem, m, p, at)
            o = h_out.at[lax.rem(m, OUTS), at] if out else None
            forward(h_v.at[m, at], wg, wu, wd, si_v.at[slot, at], m_v.at[slot, at], hid_v.at[slot, at], o)

            @pl.when(me < stages - 1)
            def _():
                send_h(m, p, at).start()

        @pl.when(m == 0)
        def _():
            pl.loop(0, FILL)(lambda p: piece(p, FILL, True))

        @pl.when((m > 0) & (me < stages - 1))
        def _():
            piece(0, 1, True)

        @pl.when((m > 0) & last)
        def _():
            piece(0, 1, False)

        @pl.when(spill)
        def _():
            for copy in spill_out(m):
                copy.start()

    def do_backward(m):
        slot = jnp.where(spill, 1 + lax.rem(m, 2), lax.rem(m, SLOTS))

        @pl.when(spill)
        def _():
            @pl.when(m == 0)
            def _():
                for copy in spill_in(0):
                    copy.start()

            for copy in spill_in(m):
                copy.wait()

            @pl.when(m + 1 < micro)
            def _():
                for copy in spill_in(m + 1):
                    copy.start()

        def piece(p, count, through):
            size = rows // count
            at = pl.ds(pl.multiple_of(p * size, size), size)
            arrived(g_v, g_sem, m, p, at)
            backward(h_v.at[m, at], g_v.at[m, at], wg, wu, wd, si_v.at[slot, at], m_v.at[slot, at],
                     dg_v.at[at], du_v.at[at], at_v.at[:, at], gt_v.at[:, at], through)
            if through:
                send_g(m, p, at).start()

        @pl.when((me > 0) & (m == micro - 1))
        def _():
            pl.loop(0, DRAIN)(lambda p: piece(p, DRAIN, True))

        @pl.when((me > 0) & (m < micro - 1))
        def _():
            piece(0, 1, True)

        @pl.when(first & (m == micro - 1))
        def _():
            pl.loop(0, DRAIN)(lambda p: piece(p, DRAIN, False))

        @pl.when(first & (m < micro - 1))
        def _():
            piece(0, 1, False)

        weights_term(acc_g, at_v, dg_v)
        weights_term(acc_u, at_v, du_v)
        weights_term(acc_d, gt_v, hid_v.at[slot])

    @pl.loop(0, micro + ahead - 1)
    def _(t):
        @pl.when(t < micro)
        def _():
            do_forward(t)

        @pl.when(spill & (t == micro))
        def _():
            for copy in spill_out(micro - 1):
                copy.wait()

        @pl.when(t >= ahead - 1)
        def _():
            do_backward(t - ahead + 1)

    wg[...] = acc_g[...].astype(bf16)
    outs = [pltpu.make_async_copy(b, a.at[0], o_sem.at[i]) for i, (a, b) in enumerate(((og, wg), (ou, wu), (od, wd)))]
    outs[0].start()
    wu[...] = acc_u[...].astype(bf16)
    outs[1].start()
    wd[...] = acc_d[...].astype(bf16).T
    outs[2].start()

    @pl.when(me < stages - 1)
    def _():
        for m in range(micro - OUTS, micro):
            send_h(m, 0, whole).wait_send()

    @pl.when(me > 0)
    def _():
        for m in range(micro):
            send_g(m, 0, whole).wait_send()

    for out in outs:
        out.wait()


def solution(mesh):
    stages = mesh.shape["pp"]

    def step(x, dy, w_gate, w_up, w_down):
        micro, rows, d = x.shape
        ff = w_gate.shape[2]
        hbm, vmem, dma = pl.BlockSpec(memory_space=pl.ANY), pltpu.VMEM, pltpu.SemaphoreType.DMA
        outs = pl.pallas_call(
            functools.partial(kernel, stages),
            out_shape=(
                jax.ShapeDtypeStruct(w_gate.shape, bf16),
                jax.ShapeDtypeStruct(w_up.shape, bf16),
                jax.ShapeDtypeStruct(w_down.shape, bf16),
                jax.ShapeDtypeStruct((micro, rows, ff), f32),
                jax.ShapeDtypeStruct((micro, rows, ff), f32),
                jax.ShapeDtypeStruct((micro, rows, ff), bf16),
            ),
            in_specs=[hbm] * 5,
            out_specs=(hbm,) * 6,
            scratch_shapes=[
                vmem((d, ff), bf16), vmem((d, ff), bf16), vmem((ff, d), bf16),
                vmem((d, ff), f32), vmem((d, ff), f32), vmem((d, ff), f32),
                vmem((micro, rows, d), bf16), vmem((micro, rows, d), bf16), vmem((OUTS, rows, d), bf16),
                vmem((SLOTS, rows, ff), f32), vmem((SLOTS, rows, ff), f32), vmem((SLOTS, rows, ff), bf16),
                vmem((rows, ff), bf16), vmem((rows, ff), bf16), vmem((d, rows), bf16), vmem((d, rows), bf16),
                dma((3,)), dma((micro, PIECES)), dma((micro, PIECES)), dma((OUTS,)), dma((micro,)), dma((3,)), dma((2, 3)), dma((3,)),
            ],
            compiler_params=pltpu.CompilerParams(collective_id=0, has_side_effects=True, vmem_limit_bytes=67043328),
        )(x, dy, w_gate, w_up, w_down)
        return outs[:3]

    return jax.shard_map(
        step,
        mesh=mesh,
        in_specs=(P("rep", None, None),) * 2 + (P("pp", None, None),) * 3,
        out_specs=(P(("rep", "pp"), None, None),) * 3,
        check_vma=False,
    )
```

time: 1200 us -> 391 us (0.33)
  the two profiles are of different devices: /device:TPU:5 before, /device:TPU:0 now
where the time goes in v1:
time: 391 us
  Pallas kernels  384 us (98%)
  local copies, waits for them, and re-layouts  5.89 us (2%)
    pallas_call x1, Pallas kernels, step(): pl.pallas_call(functools.partial(kernel, stages), out_shape=(jax.ShapeDty...  384 us

profile of v1, /device:TPU:0, one launch (start us, length us, event | category | flops | bytes accessed | tf_op | source)
XLA Modules:
  0.0 390.8 jit_solution(12910283305113725345)
XLA Ops:
  0.6 384.2 %shard_map.76 = (bf16[1,512,1536]{2,1,0:T(8,128)(2,1)}, bf16[1,512,1536]{2,1,0:T(8,128)(2,1)}, bf16[1,1536,512]{2,1,0:T(8,128)(2,1)}, f32[16,512,1536]{2,1,0:T(8...) custom-call(bf16[16,512,512]{2,1,0:T(8,128)(2,1)} %x.1, bf16[16,512,512]{2,1,0:T(8,128)(2,1)} %dy.1, ...), custom_call_target="tpu_custom_call" | custom-call | tf_op jit(solution)/shard_map/pallas_call | solution.py:280
  384.9 0.0 copy-start.1
  384.9 2.8 copy.11
  387.7 0.0 copy-done.1
  387.7 0.0 copy-start
  387.7 1.1 copy.12
  388.8 0.8 copy-done
  389.6 1.1 copy.13
Async XLA Ops:
  384.9 2.8 copy-start.1
  387.7 2.0 copy-start

commit v2 on v1

v2 whole, which is shorter than its diff:
```python
import functools

import jax
import jax.numpy as jnp
from jax import lax
from jax.experimental import pallas as pl
from jax.experimental.pallas import tpu as pltpu
from jax.sharding import PartitionSpec as P

f32, bf16 = jnp.float32, jnp.bfloat16
SLOTS = 3
OUTS = 4
PIECES = 2
TURN_H, VIA_H, TURN_G, VIA_G = 3, 0, 4, 7
CODES_H = (3, 5, 7, 9, 11, 13, 15, 17, 19, 21, 23, 25, 27, 29)
CODES_G = (3, 5, 7, 9, 11, 13, 15, 17, 19, 21, 23, 25, 27)
LENGTHS = [94, 80, 80, 80, 80, 80, 80, 93]
TABLE = (
    (0, 201523392, 503807936, 963472743, 374957463, 374957462, 150),
    (0, 335544320, 426082656, 426088025, 426088025, 601, 0),
    (0, 406921488, 541462928, 426087941, 426088025, 601, 0),
    (0, 26219076, 92561689, 426082656, 426088025, 601, 0),
    (17039360, 23355654, 23091222, 5396502, 426088024, 601, 0),
    (76562432, 408437136, 404099460, 76940673, 426087937, 601, 0),
    (403972416, 404096385, 404096385, 404096385, 404095329, 601, 0),
    (86067280, 339304536, 240182578, 348734356, 240330034, 503800020, 57),
)
TILE = 256


def dot(a, b):
    return jnp.dot(a, b, preferred_element_type=f32)


def dot_t(a, b):
    return lax.dot_general(a, b, (((1,), (1,)), ((), ())), preferred_element_type=f32)


def normed(h):
    wide = h.astype(f32)
    scale = lax.rsqrt(jnp.mean(wide * wide, -1, keepdims=True) + 1e-6)
    return wide, scale


def forward(h_ref, wg, wu, wd, si_ref, m_ref, hid_ref, out_ref):
    wide, scale = normed(h_ref[...])
    a = (wide * scale).astype(bf16)
    for j in range(wg.shape[1] // TILE):
        cs = pl.ds(j * TILE, TILE)
        g, u = dot(a, wg[:, cs]), dot(a, wu[:, cs])
        s = 1.0 / (1.0 + jnp.exp(-g))
        si = g * s
        si_ref[:, cs] = si
        m_ref[:, cs] = u * (s + si * (1.0 - s))
        hid_ref[:, cs] = (si * u).astype(bf16)
    if out_ref is not None:
        for j in range(wd.shape[1] // TILE):
            cs = pl.ds(j * TILE, TILE)
            out_ref[:, cs] = h_ref[:, cs] + dot(hid_ref[...], wd[:, cs]).astype(bf16)


def backward(h_ref, dy_ref, wg, wu, wd, si_ref, m_ref, dg_ref, du_ref, at_ref, gt_ref, through):
    dy = dy_ref[...]
    for j in range(wg.shape[1] // TILE):
        cs = pl.ds(j * TILE, TILE)
        dh = dot_t(dy, wd[cs, :]).astype(bf16).astype(f32)
        dg_ref[:, cs] = (dh * m_ref[:, cs]).astype(bf16)
        du_ref[:, cs] = (dh * si_ref[:, cs]).astype(bf16)
    wide, scale = normed(h_ref[...])
    at_ref[...] = (wide * scale).astype(bf16).T
    gt_ref[...] = dy.T
    if through:
        da = dot_t(dg_ref[...], wg[...]).astype(bf16) + dot_t(du_ref[...], wu[...]).astype(bf16)
        da = da.astype(f32)
        c = jnp.mean(da * wide, -1, keepdims=True) * (scale * scale)
        dy_ref[...] = dy + (scale * (da - wide * c)).astype(bf16)


def weights_term(acc, left, right):
    for j in range(right.shape[1] // TILE):
        cs = pl.ds(j * TILE, TILE)
        acc[:, cs] += dot(left[...], right[:, cs]).astype(bf16).astype(f32)


def pick(index, values):
    out = values[-1]
    for i in range(len(values) - 2, -1, -1):
        out = jnp.where(index == i, values[i], out)
    return jnp.int32(out)


def kernel(stages, x, dy, wg_h, wu_h, wd_h, og, ou, od, si_h, m_h, hid_h, relay,
           wg, wu, wd, acc_g, acc_u, acc_d, h_v, g_v, h_out, si_v, m_v, hid_v, dg_v, du_v, at_v, gt_v,
           w_sem, h_sem, g_sem, hs_sem, gs_sem, out_sem, in_sem, o_sem, rr_sem, rs_sem):
    me = lax.axis_index("pp")
    micro, rows = x.shape[0], x.shape[1]
    size = rows // PIECES
    first, last = me == 0, me == stages - 1
    spill = me < stages - 2

    barrier = pltpu.get_barrier_semaphore()
    for peer in range(stages - 1):
        to = lax.rem(me + peer + 1, stages)
        pl.semaphore_signal(barrier, inc=1, device_id={"pp": to}, device_id_type=pl.DeviceIdType.MESH)

    loads = [pltpu.make_async_copy(a.at[0], b, w_sem.at[i]) for i, (a, b) in enumerate(((wg_h, wg), (wu_h, wu), (wd_h, wd)))]

    def load_pieces(m, src, to, sem):
        for p in range(PIECES):
            at = pl.ds(p * size, size)
            pltpu.make_async_copy(src.at[m, at], to.at[m, at], sem.at[m, p]).start()

    @pl.when(first)
    def _():
        load_pieces(0, x, h_v, h_sem)

    for load in loads:
        load.start()

    @pl.when(first)
    def _():
        @pl.loop(1, micro)
        def _(m):
            load_pieces(m, x, h_v, h_sem)

    @pl.when(last)
    def _():
        @pl.loop(0, micro)
        def _(m):
            load_pieces(m, dy, g_v, g_sem)

    for acc in (acc_g, acc_u, acc_d):
        acc[...] = jnp.zeros_like(acc)
    for load in loads:
        load.wait()
    pl.semaphore_wait(barrier, stages - 1)

    def arrived(buf, sem, m, p, at):
        pltpu.make_async_copy(buf.at[m, at], buf.at[m, at], sem.at[m, p]).wait()

    def remote(src, dst, send, recv, to):
        return pltpu.make_async_remote_copy(src, dst, send, recv, device_id={"pp": to}, device_id_type=pl.DeviceIdType.MESH)

    def relayed(codes, m, p):
        return functools.reduce(jnp.logical_or, [m * PIECES + p == c for c in codes], False)

    def pass_on(src, m, p, at, send, dst, recv, to, turn, via, codes):
        detour = (me == turn) & relayed(codes, m, p) if codes else False

        @pl.when(jnp.logical_not(detour))
        def _():
            remote(src, dst.at[m, at], send, recv.at[m, p], to).start()

        if codes:
            @pl.when(detour)
            def _():
                remote(src, relay.at[m * PIECES + p], send, rr_sem.at[m * PIECES + p], via).start()

    def sent_h(m):
        o = lax.rem(m, OUTS)
        remote(h_out.at[o], h_v.at[m], hs_sem.at[o], h_sem.at[m, 0], me + 1).wait_send()

    saved = ((si_v, si_h), (m_v, m_h), (hid_v, hid_h))

    def spill_out(m, p, at):
        return [pltpu.make_async_copy(v.at[0, at], h.at[m, at], out_sem.at[p, i]) for i, (v, h) in enumerate(saved)]

    def spill_in(m):
        slot = lax.rem(m, 2)
        return [pltpu.make_async_copy(h.at[m], v.at[1 + slot], in_sem.at[slot, i]) for i, (v, h) in enumerate(saved)]

    def rows_of(p):
        return pl.ds(pl.multiple_of(p * size, size), size)

    def do_forward(n, fetched):
        m, p = lax.div(n, PIECES), lax.rem(n, PIECES)
        at = rows_of(p)
        slot = jnp.where(spill, 0, lax.rem(m, SLOTS))

        @pl.when(spill & (m > 0) & (fetched < m))
        def _():
            for copy in spill_out(m - 1, p, at):
                copy.wait()

        @pl.when((p == 0) & (m >= OUTS) & (me < stages - 1))
        def _():
            sent_h(m - OUTS)

        arrived(h_v, h_sem, m, p, at)
        keep = si_v.at[slot, at], m_v.at[slot, at], hid_v.at[slot, at]

        @pl.when(me < stages - 1)
        def _():
            o = lax.rem(m, OUTS)
            forward(h_v.at[m, at], wg, wu, wd, *keep, h_out.at[o, at])
            pass_on(h_out.at[o, at], m, p, at, hs_sem.at[o], h_v, h_sem, me + 1, TURN_H, VIA_H, CODES_H)

        @pl.when(last)
        def _():
            forward(h_v.at[m, at], wg, wu, wd, *keep, None)

        @pl.when(spill)
        def _():
            for copy in spill_out(m, p, at):
                copy.start()

    def fetch(m, forwards):
        for p in range(PIECES):
            @pl.when(forwards <= (m + 1) * PIECES + p)
            def _():
                for copy in spill_out(m, p, pl.ds(p * size, size)):
                    copy.wait()

        for copy in spill_in(m):
            copy.start()

    def do_backward(n, forwards, fetched):
        m, p = lax.div(n, PIECES), lax.rem(n, PIECES)
        at = rows_of(p)
        slot = jnp.where(spill, 1 + lax.rem(m, 2), lax.rem(m, SLOTS))

        @pl.when(spill & (p == 0))
        def _():
            @pl.when(fetched <= m)
            def _():
                fetch(m, forwards)

            for copy in spill_in(m):
                copy.wait()

            @pl.when((m + 1 < micro) & (forwards >= (m + 2) * PIECES))
            def _():
                fetch(m + 1, forwards)

        arrived(g_v, g_sem, m, p, at)

        def work(through):
            backward(h_v.at[m, at], g_v.at[m, at], wg, wu, wd, si_v.at[slot, at], m_v.at[slot, at],
                     dg_v.at[at], du_v.at[at], at_v.at[:, at], gt_v.at[:, at], through)

        @pl.when(me > 0)
        def _():
            work(True)
            pass_on(g_v.at[m, at], m, p, at, gs_sem.at[m], g_v, g_sem, me - 1, TURN_G, VIA_G, CODES_G)

        @pl.when(first)
        def _():
            work(False)

    def do_weights(m):
        slot = jnp.where(spill, 1 + lax.rem(m, 2), lax.rem(m, SLOTS))
        weights_term(acc_g, at_v, dg_v)
        weights_term(acc_u, at_v, du_v)
        weights_term(acc_d, gt_v, hid_v.at[slot])

    def do_relay(n):
        def hop(codes, dst, recv, to):
            c = pick(n, codes)
            m, p = lax.div(c, PIECES), lax.rem(c, PIECES)
            pltpu.make_async_copy(relay.at[c], relay.at[c], rr_sem.at[c]).wait()
            remote(relay.at[c], dst.at[m, rows_of(p)], rs_sem.at[c], recv.at[m, p], to).start()

        if CODES_H:
            @pl.when(me == VIA_H)
            def _():
                hop(CODES_H, h_v, h_sem, TURN_H + 1)

        if CODES_G:
            @pl.when(me == VIA_G)
            def _():
                hop(CODES_G, g_v, g_sem, TURN_G - 1)

    total = pick(me, LENGTHS)
    words = len(TABLE[0])

    def block(w, carry):
        word = pick(w, [pick(me, [row[i] for row in TABLE]) for i in range(words)])

        def turn(_, carry):
            word, nf, nb, nw, nr, fetched = carry
            op = lax.rem(word, 4)

            @pl.when(op == 0)
            def _():
                do_forward(nf, fetched)

            @pl.when(op == 1)
            def _():
                do_backward(nb, nf, fetched)

            @pl.when(op == 2)
            def _():
                do_weights(nw)

            if CODES_H or CODES_G:
                @pl.when(op == 3)
                def _():
                    do_relay(nr)

            m = lax.div(nb, PIECES)
            more = jnp.where((m + 1 < micro) & (nf >= (m + 2) * PIECES), m + 2, m + 1)
            fetched = jnp.where((op == 1) & (lax.rem(nb, PIECES) == 0), more, fetched)
            one = jnp.int32(1)
            return (lax.div(word, 4), nf + jnp.where(op == 0, one, 0), nb + jnp.where(op == 1, one, 0),
                    nw + jnp.where(op == 2, one, 0), nr + jnp.where(op == 3, one, 0), fetched)

        return lax.fori_loop(0, jnp.minimum(15, total - 15 * w), turn, (word, *carry))[1:]

    lax.fori_loop(0, lax.div(total + 14, 15), block, (jnp.int32(0),) * 5)

    wg[...] = acc_g[...].astype(bf16)
    outs = [pltpu.make_async_copy(b, a.at[0], o_sem.at[i]) for i, (a, b) in enumerate(((og, wg), (ou, wu), (od, wd)))]
    outs[0].start()
    wu[...] = acc_u[...].astype(bf16)
    outs[1].start()
    wd[...] = acc_d[...].astype(bf16).T
    outs[2].start()

    @pl.when(me < stages - 1)
    def _():
        for m in range(micro - OUTS, micro):
            sent_h(m)

    @pl.when(me > 0)
    def _():
        for m in range(micro):
            remote(g_v.at[m], g_v.at[m], gs_sem.at[m], g_sem.at[m, 0], me - 1).wait_send()

    for via, codes in ((VIA_H, CODES_H), (VIA_G, CODES_G)):
        @pl.when(me == via)
        def _():
            for c in codes:
                remote(relay.at[c], relay.at[c], rs_sem.at[c], rr_sem.at[c], TURN_H).wait_send()

    for out in outs:
        out.wait()


def solution(mesh):
    stages = mesh.shape["pp"]

    def step(x, dy, w_gate, w_up, w_down):
        micro, rows, d = x.shape
        ff = w_gate.shape[2]
        hbm, vmem, dma = pl.BlockSpec(memory_space=pl.ANY), pltpu.VMEM, pltpu.SemaphoreType.DMA
        outs = pl.pallas_call(
            functools.partial(kernel, stages),
            out_shape=(
                jax.ShapeDtypeStruct(w_gate.shape, bf16),
                jax.ShapeDtypeStruct(w_up.shape, bf16),
                jax.ShapeDtypeStruct(w_down.shape, bf16),
                jax.ShapeDtypeStruct((micro, rows, ff), f32),
                jax.ShapeDtypeStruct((micro, rows, ff), f32),
                jax.ShapeDtypeStruct((micro, rows, ff), bf16),
                jax.ShapeDtypeStruct((micro * PIECES, rows // PIECES, d), bf16),
            ),
            in_specs=[hbm] * 5,
            out_specs=(hbm,) * 7,
            scratch_shapes=[
                vmem((d, ff), bf16), vmem((d, ff), bf16), vmem((ff, d), bf16),
                vmem((d, ff), f32), vmem((d, ff), f32), vmem((d, ff), f32),
                vmem((micro, rows, d), bf16), vmem((micro, rows, d), bf16), vmem((OUTS, rows, d), bf16),
                vmem((SLOTS, rows, ff), f32), vmem((SLOTS, rows, ff), f32), vmem((SLOTS, rows, ff), bf16),
                vmem((rows, ff), bf16), vmem((rows, ff), bf16), vmem((d, rows), bf16), vmem((d, rows), bf16),
                dma((3,)), dma((micro, PIECES)), dma((micro, PIECES)), dma((OUTS,)), dma((micro,)), dma((PIECES, 3)), dma((2, 3)), dma((3,)),
                dma((micro * PIECES,)), dma((micro * PIECES,)),
            ],
            compiler_params=pltpu.CompilerParams(collective_id=0, has_side_effects=True, vmem_limit_bytes=67043328),
        )(x, dy, w_gate, w_up, w_down)
        return outs[:3]

    return jax.shard_map(
        step,
        mesh=mesh,
        in_specs=(P("rep", None, None),) * 2 + (P("pp", None, None),) * 3,
        out_specs=(P(("rep", "pp"), None, None),) * 3,
        check_vma=False,
    )
```

time: 391 us -> 239 us (0.61)
  Pallas kernels: 384 us -> 232 us
    pallas_call x1, Pallas kernels: 384 us -> 232 us  [step(): pl.pallas_call(functools.partial(kernel, stages), out_shape=(jax.ShapeDty...]
where the time goes in v2:
time: 239 us
  Pallas kernels  232 us (97%)
  local copies, waits for them, and re-layouts  5.89 us (2%)
    pallas_call x1, Pallas kernels, step(): pl.pallas_call(functools.partial(kernel, stages), out_shape=(jax.ShapeDty...  232 us
    unnamed x7, local copies, waits for them, and re-layouts  5.89 us

profile of v2, /device:TPU:0, one launch (start us, length us, event | category | flops | bytes accessed | tf_op | source)
XLA Modules:
  0.0 238.7 jit_solution(12027351353071556680)
XLA Ops:
  0.6 232.2 %shard_map.76 = (bf16[1,512,1536]{2,1,0:T(8,128)(2,1)}, bf16[1,512,1536]{2,1,0:T(8,128)(2,1)}, bf16[1,1536,512]{2,1,0:T(8,128)(2,1)}, f32[16,512,1536]{2,1,0:T(8...) custom-call(bf16[16,512,512]{2,1,0:T(8,128)(2,1)} %x.1, ...), custom_call_target="tpu_custom_call" | custom-call | tf_op jit(solution)/shard_map/pallas_call | solution.py:346
  232.8 0.0 copy-start.1
  232.8 2.8 %copy.11 = bf16[1,512,1536]{2,1,0:T(8,128)(2,1)} copy(bf16[1,512,1536]{2,1,0:T(8,128)(2,1)} %get-tuple-element.12) | data formatting | bytes 3145728
  235.6 0.0 copy-done.1
  235.6 0.0 copy-start
  235.6 1.1 copy.12
  236.8 0.8 copy-done
  237.6 1.1 copy.13
Async XLA Ops:
  232.8 2.8 %copy-start.1 = (bf16[1,512,1536]{2,1,0:T(8,128)(2,1)S(1)}, bf16[1,512,1536]{2,1,0:T(8,128)(2,1)}, u32[]{:S(2)}) copy-start(bf16[1,512,1536]{2,1,0:T(8,128)(2,1)} %get-tuple-element.13) | copy-start | bytes 4718596
  235.6 2.0 copy-start

commit v3 on v2

--- a/solution.py
+++ b/solution.py
@@ -9,31 +9,28 @@
 
 f32, bf16 = jnp.float32, jnp.bfloat16
 SLOTS = 3
-OUTS = 4
+OUTS = 3
 PIECES = 2
+FINE = 4
 TURN_H, VIA_H, TURN_G, VIA_G = 3, 0, 4, 7
-CODES_H = (3, 5, 7, 9, 11, 13, 15, 17, 19, 21, 23, 25, 27, 29)
-CODES_G = (3, 5, 7, 9, 11, 13, 15, 17, 19, 21, 23, 25, 27)
-LENGTHS = [94, 80, 80, 80, 80, 80, 80, 93]
+CODES_H = (10, 12, 13, 14, 15, 16, 17, 18, 20, 21, 25, 30, 31)
+CODES_G = (0, 2, 4, 5, 6, 8, 11, 13, 14, 16)
+LENGTHS = [97, 84, 84, 84, 84, 84, 84, 94]
 TABLE = (
-    (0, 201523392, 503807936, 963472743, 374957463, 374957462, 150),
-    (0, 335544320, 426082656, 426088025, 426088025, 601, 0),
-    (0, 406921488, 541462928, 426087941, 426088025, 601, 0),
-    (0, 26219076, 92561689, 426082656, 426088025, 601, 0),
-    (17039360, 23355654, 23091222, 5396502, 426088024, 601, 0),
-    (76562432, 408437136, 404099460, 76940673, 426087937, 601, 0),
-    (403972416, 404096385, 404096385, 404096385, 404095329, 601, 0),
-    (86067280, 339304536, 240182578, 348734356, 240330034, 503800020, 57),
+    (0, 1069547520, 31328223, 629241878, 426108773, 426088025, 9561),
+    (0, 155189248, 423772564, 374957441, 374957462, 152982, 0),
+    (0, 84415488, 92364888, 374886994, 374957462, 152982, 0),
+    (0, 542146880, 542643792, 370447889, 374957462, 152982, 0),
+    (17825792, 345374994, 157287808, 101810533, 374887001, 152982, 0),
+    (38010880, 92280337, 402743318, 287578201, 370447894, 152982, 0),
+    (557876480, 559945236, 21501460, 23091222, 425744406, 152961, 0),
+    (403973376, 21894279, 314914934, 24646797, 283479134, 278144265, 149),
 )
 TILE = 256
 
 
 def dot(a, b):
     return jnp.dot(a, b, preferred_element_type=f32)
-
-
-def dot_t(a, b):
-    return lax.dot_general(a, b, (((1,), (1,)), ((), ())), preferred_element_type=f32)
 
 
 def normed(h):
@@ -59,18 +56,18 @@
             out_ref[:, cs] = h_ref[:, cs] + dot(hid_ref[...], wd[:, cs]).astype(bf16)
 
 
-def backward(h_ref, dy_ref, wg, wu, wd, si_ref, m_ref, dg_ref, du_ref, at_ref, gt_ref, through):
+def backward(h_ref, dy_ref, wgt, wut, wdt, si_ref, m_ref, dg_ref, du_ref, at_ref, gt_ref, through):
     dy = dy_ref[...]
-    for j in range(wg.shape[1] // TILE):
+    for j in range(wdt.shape[1] // TILE):
         cs = pl.ds(j * TILE, TILE)
-        dh = dot_t(dy, wd[cs, :]).astype(bf16).astype(f32)
+        dh = dot(dy, wdt[:, cs]).astype(bf16).astype(f32)
         dg_ref[:, cs] = (dh * m_ref[:, cs]).astype(bf16)
         du_ref[:, cs] = (dh * si_ref[:, cs]).astype(bf16)
     wide, scale = normed(h_ref[...])
     at_ref[...] = (wide * scale).astype(bf16).T
     gt_ref[...] = dy.T
     if through:
-        da = dot_t(dg_ref[...], wg[...]).astype(bf16) + dot_t(du_ref[...], wu[...]).astype(bf16)
+        da = dot(dg_ref[...], wgt[...]).astype(bf16) + dot(du_ref[...], wut[...]).astype(bf16)
         da = da.astype(f32)
         c = jnp.mean(da * wide, -1, keepdims=True) * (scale * scale)
         dy_ref[...] = dy + (scale * (da - wide * c)).astype(bf16)
@@ -90,7 +87,7 @@
 
 
 def kernel(stages, x, dy, wg_h, wu_h, wd_h, og, ou, od, si_h, m_h, hid_h, relay,
-           wg, wu, wd, acc_g, acc_u, acc_d, h_v, g_v, h_out, si_v, m_v, hid_v, dg_v, du_v, at_v, gt_v,
+           wg, wu, wd, wgt, wut, wdt, acc_g, acc_u, acc_d, h_v, g_v, h_out, si_v, m_v, hid_v, dg_v, du_v, at_v, gt_v,
            w_sem, h_sem, g_sem, hs_sem, gs_sem, out_sem, in_sem, o_sem, rr_sem, rs_sem):
     me = lax.axis_index("pp")
     micro, rows = x.shape[0], x.shape[1]
@@ -105,14 +102,14 @@
 
     loads = [pltpu.make_async_copy(a.at[0], b, w_sem.at[i]) for i, (a, b) in enumerate(((wg_h, wg), (wu_h, wu), (wd_h, wd)))]
 
-    def load_pieces(m, src, to, sem):
-        for p in range(PIECES):
-            at = pl.ds(p * size, size)
+    def load_pieces(m, src, to, sem, count=PIECES):
+        for p in range(count):
+            at = pl.ds(p * (rows // count), rows // count)
             pltpu.make_async_copy(src.at[m, at], to.at[m, at], sem.at[m, p]).start()
 
     @pl.when(first)
     def _():
-        load_pieces(0, x, h_v, h_sem)
+        load_pieces(0, x, h_v, h_sem, FINE)
 
     for load in loads:
         load.start()
@@ -125,9 +122,11 @@
 
     @pl.when(last)
     def _():
-        @pl.loop(0, micro)
+        @pl.loop(0, micro - 1)
         def _(m):
             load_pieces(m, dy, g_v, g_sem)
+
+        load_pieces(micro - 1, dy, g_v, g_sem, FINE)
 
     for acc in (acc_g, acc_u, acc_d):
         acc[...] = jnp.zeros_like(acc)
@@ -135,6 +134,12 @@
         load.wait()
     pl.semaphore_wait(barrier, stages - 1)
 
+    @pl.when(me > 0)
+    def _():
+        wgt[...] = wg[...].T
+        wut[...] = wu[...].T
+        wdt[...] = wd[...].T
+
     def arrived(buf, sem, m, p, at):
         pltpu.make_async_copy(buf.at[m, at], buf.at[m, at], sem.at[m, p]).wait()
 
@@ -169,44 +174,64 @@
         slot = lax.rem(m, 2)
         return [pltpu.make_async_copy(h.at[m], v.at[1 + slot], in_sem.at[slot, i]) for i, (v, h) in enumerate(saved)]
 
-    def rows_of(p):
+    def rows_of(p, size=size):
         return pl.ds(pl.multiple_of(p * size, size), size)
 
+    extra = FINE - PIECES
+
     def do_forward(n, fetched):
-        m, p = lax.div(n, PIECES), lax.rem(n, PIECES)
-        at = rows_of(p)
+        fine = n < FINE
+        m = jnp.where(fine, 0, lax.div(n - extra, PIECES))
+        p = jnp.where(fine, n, lax.rem(n + PIECES - extra, PIECES))
         slot = jnp.where(spill, 0, lax.rem(m, SLOTS))
+        o = lax.rem(m, OUTS)
 
         @pl.when(spill & (m > 0) & (fetched < m))
         def _():
-            for copy in spill_out(m - 1, p, at):
+            for copy in spill_out(m - 1, p, rows_of(p)):
                 copy.wait()
 
         @pl.when((p == 0) & (m >= OUTS) & (me < stages - 1))
         def _():
             sent_h(m - OUTS)
 
-        arrived(h_v, h_sem, m, p, at)
-        keep = si_v.at[slot, at], m_v.at[slot, at], hid_v.at[slot, at]
-
-        @pl.when(me < stages - 1)
-        def _():
-            o = lax.rem(m, OUTS)
-            forward(h_v.at[m, at], wg, wu, wd, *keep, h_out.at[o, at])
-            pass_on(h_out.at[o, at], m, p, at, hs_sem.at[o], h_v, h_sem, me + 1, TURN_H, VIA_H, CODES_H)
-
-        @pl.when(last)
-        def _():
-            forward(h_v.at[m, at], wg, wu, wd, *keep, None)
-
-        @pl.when(spill)
-        def _():
-            for copy in spill_out(m, p, at):
+        def work(size, codes):
+            at = rows_of(p, size)
+            arrived(h_v, h_sem, m, p, at)
+            keep = si_v.at[slot, at], m_v.at[slot, at], hid_v.at[slot, at]
+
+            @pl.when(me < stages - 1)
+            def _():
+                forward(h_v.at[m, at], wg, wu, wd, *keep, h_out.at[o, at])
+                pass_on(h_out.at[o, at], m, p, at, hs_sem.at[o], h_v, h_sem, me + 1, TURN_H, VIA_H, codes)
+
+            @pl.when(last)
+            def _():
+                forward(h_v.at[m, at], wg, wu, wd, *keep, None)
+
+        @pl.when(fine)
+        def _():
+            work(rows // FINE, ())
+
+        @pl.when(jnp.logical_not(fine))
+        def _():
+            work(size, CODES_H)
+
+        finer = FINE // PIECES
+
+        @pl.when(spill & fine & (lax.rem(n, finer) == finer - 1))
+        def _():
+            for copy in spill_out(0, lax.div(n, finer), rows_of(lax.div(n, finer))):
+                copy.start()
+
+        @pl.when(spill & jnp.logical_not(fine))
+        def _():
+            for copy in spill_out(m, p, rows_of(p)):
                 copy.start()
 
     def fetch(m, forwards):
         for p in range(PIECES):
-            @pl.when(forwards <= (m + 1) * PIECES + p)
+            @pl.when(forwards <= (m + 1) * PIECES + extra + p)
             def _():
                 for copy in spill_out(m, p, pl.ds(p * size, size)):
                     copy.wait()
@@ -215,9 +240,14 @@
             copy.start()
 
     def do_backward(n, forwards, fetched):
-        m, p = lax.div(n, PIECES), lax.rem(n, PIECES)
-        at = rows_of(p)
+        m = jnp.minimum(lax.div(n, PIECES), micro - 1)
+        p = n - m * PIECES
+        fine = m == micro - 1
         slot = jnp.where(spill, 1 + lax.rem(m, 2), lax.rem(m, SLOTS))
+
+        @pl.when(first & (n == 0))
+        def _():
+            wdt[...] = wd[...].T
 
         @pl.when(spill & (p == 0))
         def _():
@@ -228,24 +258,34 @@
             for copy in spill_in(m):
                 copy.wait()
 
-            @pl.when((m + 1 < micro) & (forwards >= (m + 2) * PIECES))
+            @pl.when((m + 1 < micro) & (forwards >= (m + 2) * PIECES + extra))
             def _():
                 fetch(m + 1, forwards)
 
-        arrived(g_v, g_sem, m, p, at)
-
-        def work(through):
-            backward(h_v.at[m, at], g_v.at[m, at], wg, wu, wd, si_v.at[slot, at], m_v.at[slot, at],
-                     dg_v.at[at], du_v.at[at], at_v.at[:, at], gt_v.at[:, at], through)
-
-        @pl.when(me > 0)
-        def _():
-            work(True)
-            pass_on(g_v.at[m, at], m, p, at, gs_sem.at[m], g_v, g_sem, me - 1, TURN_G, VIA_G, CODES_G)
-
-        @pl.when(first)
-        def _():
-            work(False)
+        def work(size, codes):
+            at = rows_of(p, size)
+            arrived(g_v, g_sem, m, p, at)
+
+            def piece(through):
+                backward(h_v.at[m, at], g_v.at[m, at], wgt, wut, wdt, si_v.at[slot, at], m_v.at[slot, at],
+                         dg_v.at[at], du_v.at[at], at_v.at[:, at], gt_v.at[:, at], through)
+
+            @pl.when(me > 0)
+            def _():
+                piece(True)
+                pass_on(g_v.at[m, at], m, p, at, gs_sem.at[m], g_v, g_sem, me - 1, TURN_G, VIA_G, codes)
+
+            @pl.when(first)
+            def _():
+                piece(False)
+
+        @pl.when(fine)
+        def _():
+            work(rows // FINE, ())
+
+        @pl.when(jnp.logical_not(fine))
+        def _():
+            work(size, CODES_G)
 
     def do_weights(m):
         slot = jnp.where(spill, 1 + lax.rem(m, 2), lax.rem(m, SLOTS))
@@ -297,9 +337,9 @@
                 def _():
                     do_relay(nr)
 
-            m = lax.div(nb, PIECES)
-            more = jnp.where((m + 1 < micro) & (nf >= (m + 2) * PIECES), m + 2, m + 1)
-            fetched = jnp.where((op == 1) & (lax.rem(nb, PIECES) == 0), more, fetched)
+            m = jnp.minimum(lax.div(nb, PIECES), micro - 1)
+            more = jnp.where((m + 1 < micro) & (nf >= (m + 2) * PIECES + extra), m + 2, m + 1)
+            fetched = jnp.where((op == 1) & (nb == m * PIECES), more, fetched)
             one = jnp.int32(1)
             return (lax.div(word, 4), nf + jnp.where(op == 0, one, 0), nb + jnp.where(op == 1, one, 0),
                     nw + jnp.where(op == 2, one, 0), nr + jnp.where(op == 3, one, 0), fetched)
@@ -358,11 +398,12 @@
             out_specs=(hbm,) * 7,
             scratch_shapes=[
                 vmem((d, ff), bf16), vmem((d, ff), bf16), vmem((ff, d), bf16),
+                vmem((ff, d), bf16), vmem((ff, d), bf16), vmem((d, ff), bf16),
                 vmem((d, ff), f32), vmem((d, ff), f32), vmem((d, ff), f32),
                 vmem((micro, rows, d), bf16), vmem((micro, rows, d), bf16), vmem((OUTS, rows, d), bf16),
                 vmem((SLOTS, rows, ff), f32), vmem((SLOTS, rows, ff), f32), vmem((SLOTS, rows, ff), bf16),
                 vmem((rows, ff), bf16), vmem((rows, ff), bf16), vmem((d, rows), bf16), vmem((d, rows), bf16),
-                dma((3,)), dma((micro, PIECES)), dma((micro, PIECES)), dma((OUTS,)), dma((micro,)), dma((PIECES, 3)), dma((2, 3)), dma((3,)),
+                dma((3,)), dma((micro, FINE)), dma((micro, FINE)), dma((OUTS,)), dma((micro,)), dma((PIECES, 3)), dma((2, 3)), dma((3,)),
                 dma((micro * PIECES,)), dma((micro * PIECES,)),
             ],
             compiler_params=pltpu.CompilerParams(collective_id=0, has_side_effects=True, vmem_limit_bytes=67043328),

time: 239 us -> 228 us (0.954)
  Pallas kernels: 232 us -> 221 us
    pallas_call x1, Pallas kernels: 232 us -> 221 us  [step(): pl.pallas_call(functools.partial(kernel, stages), out_shape=(jax.ShapeDty...]
where the time goes in v3:
time: 228 us
  Pallas kernels  221 us (97%)
  local copies, waits for them, and re-layouts  5.89 us (3%)
    pallas_call x1, Pallas kernels, step(): pl.pallas_call(functools.partial(kernel, stages), out_shape=(jax.ShapeDty...  221 us
    unnamed x7, local copies, waits for them, and re-layouts  5.89 us

profile of v3, /device:TPU:0, one launch (start us, length us, event | category | flops | bytes accessed | tf_op | source)
XLA Modules:
  0.0 227.5 jit_solution(17119222843007446762)
XLA Ops:
  0.6 221.0 %shard_map.76 = (bf16[1,512,1536]{2,1,0:T(8,128)(2,1)}, bf16[1,512,1536]{2,1,0:T(8,128)(2,1)}, bf16[1,1536,512]{2,1,0:T(8,128)(2,1)}, f32[16,512,1536]{2,1,0:T(8...) custom-call(bf16[16,512,512]{2,1,0:T(8,128)(2,1)} %x.1, ...), custom_call_target="tpu_custom_call" | custom-call | tf_op jit(solution)/shard_map/pallas_call | solution.py:386
  221.6 0.0 copy-start.1
  221.6 2.8 %copy.11 = bf16[1,512,1536]{2,1,0:T(8,128)(2,1)} copy(bf16[1,512,1536]{2,1,0:T(8,128)(2,1)} %get-tuple-element.12) | data formatting | bytes 3145728
  224.4 0.0 copy-done.1
  224.4 0.0 copy-start
  224.4 1.1 copy.12
  225.5 0.8 copy-done
  226.4 1.1 copy.13
Async XLA Ops:
  221.6 2.8 %copy-start.1 = (bf16[1,512,1536]{2,1,0:T(8,128)(2,1)S(1)}, bf16[1,512,1536]{2,1,0:T(8,128)(2,1)}, u32[]{:S(2)}) copy-start(bf16[1,512,1536]{2,1,0:T(8,128)(2,1)} %get-tuple-element.13) | copy-start | bytes 4718596
  224.4 2.0 copy-start

commit v4 on v3

--- a/solution.py
+++ b/solution.py
@@ -12,19 +12,20 @@
 OUTS = 3
 PIECES = 2
 FINE = 4
+EARLY, LATE = 3, 3
 TURN_H, VIA_H, TURN_G, VIA_G = 3, 0, 4, 7
-CODES_H = (10, 12, 13, 14, 15, 16, 17, 18, 20, 21, 25, 30, 31)
-CODES_G = (0, 2, 4, 5, 6, 8, 11, 13, 14, 16)
-LENGTHS = [97, 84, 84, 84, 84, 84, 84, 94]
+CODES_H = (8, 9, 10, 11, 13, 17, 18, 20, 21, 23, 24, 25, 28, 30, 31)
+CODES_G = (0, 3, 5, 6, 10, 14, 15, 17)
+LENGTHS = [107, 92, 92, 92, 92, 92, 92, 100]
 TABLE = (
-    (0, 1069547520, 31328223, 629241878, 426108773, 426088025, 9561),
-    (0, 155189248, 423772564, 374957441, 374957462, 152982, 0),
-    (0, 84415488, 92364888, 374886994, 374957462, 152982, 0),
-    (0, 542146880, 542643792, 370447889, 374957462, 152982, 0),
-    (17825792, 345374994, 157287808, 101810533, 374887001, 152982, 0),
-    (38010880, 92280337, 402743318, 287578201, 370447894, 152982, 0),
-    (557876480, 559945236, 21501460, 23091222, 425744406, 152961, 0),
-    (403973376, 21894279, 314914934, 24646797, 283479134, 278144265, 149),
+    (0, 0, 98621439, 31327724, 395730523, 426088030, 362112345, 9),
+    (0, 0, 307270693, 426083428, 426088025, 362112345, 9, 0),
+    (0, 100990976, 140001668, 102110341, 426088025, 362112345, 9, 0),
+    (0, 274808832, 369435654, 293962080, 426088006, 362112345, 9, 0),
+    (268435456, 92291460, 23091288, 5788248, 307779606, 362112345, 9, 0),
+    (335544320, 541139992, 404100613, 101815812, 370541956, 362112326, 9, 0),
+    (537198592, 38806917, 542246277, 139986309, 542639493, 361060437, 9, 0),
+    (23069952, 940892512, 87610405, 344318034, 561125296, 369448980, 611461, 0),
 )
 TILE = 256
 
@@ -116,17 +117,21 @@
 
     @pl.when(first)
     def _():
-        @pl.loop(1, micro)
+        for m in range(1, EARLY):
+            load_pieces(m, x, h_v, h_sem, FINE)
+
+        @pl.loop(EARLY, micro)
         def _(m):
             load_pieces(m, x, h_v, h_sem)
 
     @pl.when(last)
     def _():
-        @pl.loop(0, micro - 1)
+        @pl.loop(0, micro - LATE)
         def _(m):
             load_pieces(m, dy, g_v, g_sem)
 
-        load_pieces(micro - 1, dy, g_v, g_sem, FINE)
+        for m in range(micro - LATE, micro):
+            load_pieces(m, dy, g_v, g_sem, FINE)
 
     for acc in (acc_g, acc_u, acc_d):
         acc[...] = jnp.zeros_like(acc)
@@ -147,7 +152,10 @@
         return pltpu.make_async_remote_copy(src, dst, send, recv, device_id={"pp": to}, device_id_type=pl.DeviceIdType.MESH)
 
     def relayed(codes, m, p):
-        return functools.reduce(jnp.logical_or, [m * PIECES + p == c for c in codes], False)
+        low, high = (sum(1 << c % 16 for c in codes if c // 16 == part) for part in range(2))
+        code = m * PIECES + p
+        word = jnp.where(code < 16, low, high)
+        return lax.rem(lax.shift_right_logical(jnp.int32(word), lax.rem(code, 16)), 2) == 1
 
     def pass_on(src, m, p, at, send, dst, recv, to, turn, via, codes):
         detour = (me == turn) & relayed(codes, m, p) if codes else False
@@ -177,18 +185,25 @@
     def rows_of(p, size=size):
         return pl.ds(pl.multiple_of(p * size, size), size)
 
-    extra = FINE - PIECES
+    finer = FINE // PIECES
+
+    def steps_before(m):
+        return m * PIECES + jnp.minimum(m, EARLY) * (FINE - PIECES)
 
     def do_forward(n, fetched):
-        fine = n < FINE
-        m = jnp.where(fine, 0, lax.div(n - extra, PIECES))
-        p = jnp.where(fine, n, lax.rem(n + PIECES - extra, PIECES))
+        fine = n < FINE * EARLY
+        coarse = jnp.maximum(n - FINE * EARLY, 0)
+        m = jnp.where(fine, lax.div(n, FINE), EARLY + lax.div(coarse, PIECES))
+        p = jnp.where(fine, lax.rem(n, FINE), lax.rem(coarse, PIECES))
+        half = jnp.where(fine, lax.div(p, finer), p)
+        opens = jnp.logical_not(fine) | (lax.rem(p, finer) == 0)
+        closes = jnp.logical_not(fine) | (lax.rem(p, finer) == finer - 1)
         slot = jnp.where(spill, 0, lax.rem(m, SLOTS))
         o = lax.rem(m, OUTS)
 
-        @pl.when(spill & (m > 0) & (fetched < m))
-        def _():
-            for copy in spill_out(m - 1, p, rows_of(p)):
+        @pl.when(spill & opens & (m > 0) & (fetched < m))
+        def _():
+            for copy in spill_out(m - 1, half, rows_of(half)):
                 copy.wait()
 
         @pl.when((p == 0) & (m >= OUTS) & (me < stages - 1))
@@ -217,21 +232,14 @@
         def _():
             work(size, CODES_H)
 
-        finer = FINE // PIECES
-
-        @pl.when(spill & fine & (lax.rem(n, finer) == finer - 1))
-        def _():
-            for copy in spill_out(0, lax.div(n, finer), rows_of(lax.div(n, finer))):
-                copy.start()
-
-        @pl.when(spill & jnp.logical_not(fine))
-        def _():
-            for copy in spill_out(m, p, rows_of(p)):
+        @pl.when(spill & closes)
+        def _():
+            for copy in spill_out(m, half, rows_of(half)):
                 copy.start()
 
     def fetch(m, forwards):
         for p in range(PIECES):
-            @pl.when(forwards <= (m + 1) * PIECES + extra + p)
+            @pl.when(forwards <= steps_before(m + 1) + p * jnp.where(m + 1 < EARLY, finer, 1))
             def _():
                 for copy in spill_out(m, p, pl.ds(p * size, size)):
                     copy.wait()
@@ -240,9 +248,10 @@
             copy.start()
 
     def do_backward(n, forwards, fetched):
-        m = jnp.minimum(lax.div(n, PIECES), micro - 1)
-        p = n - m * PIECES
-        fine = m == micro - 1
+        fine = n >= (micro - LATE) * PIECES
+        late = jnp.maximum(n - (micro - LATE) * PIECES, 0)
+        m = jnp.where(fine, micro - LATE + lax.div(late, FINE), lax.div(n, PIECES))
+        p = jnp.where(fine, lax.rem(late, FINE), lax.rem(n, PIECES))
         slot = jnp.where(spill, 1 + lax.rem(m, 2), lax.rem(m, SLOTS))
 
         @pl.when(first & (n == 0))
@@ -258,7 +267,7 @@
             for copy in spill_in(m):
                 copy.wait()
 
-            @pl.when((m + 1 < micro) & (forwards >= (m + 2) * PIECES + extra))
+            @pl.when((m + 1 < micro) & (forwards >= steps_before(m + 2)))
             def _():
                 fetch(m + 1, forwards)
 
@@ -337,9 +346,11 @@
                 def _():
                     do_relay(nr)
 
-            m = jnp.minimum(lax.div(nb, PIECES), micro - 1)
-            more = jnp.where((m + 1 < micro) & (nf >= (m + 2) * PIECES + extra), m + 2, m + 1)
-            fetched = jnp.where((op == 1) & (nb == m * PIECES), more, fetched)
+            late = jnp.maximum(nb - (micro - LATE) * PIECES, 0)
+            m = jnp.where(late > 0, micro - LATE + lax.div(late, FINE), lax.div(nb, PIECES))
+            more = jnp.where((m + 1 < micro) & (nf >= steps_before(m + 2)), m + 2, m + 1)
+            begins = jnp.where(late > 0, lax.rem(late, FINE), lax.rem(nb, PIECES)) == 0
+            fetched = jnp.where((op == 1) & begins, more, fetched)
             one = jnp.int32(1)
             return (lax.div(word, 4), nf + jnp.where(op == 0, one, 0), nb + jnp.where(op == 1, one, 0),
                     nw + jnp.where(op == 2, one, 0), nr + jnp.where(op == 3, one, 0), fetched)
@@ -374,6 +385,22 @@
 
     for out in outs:
         out.wait()
+
+
+def settle(a, b, c, oa, ob, oc, va, vb, vc, in_sem, out_sem):
+    todo = []
+    for i, (src, via, dst) in enumerate(((a, va, oa), (b, vb, ob), (c, vc, oc))):
+        half = src.shape[1] // 2
+        for p in range(2):
+            at = pl.ds(p * half, half)
+            todo.append((pltpu.make_async_copy(src.at[0, at], via.at[at], in_sem.at[i, p]), pltpu.make_async_copy(via.at[at], dst.at[0, at], out_sem.at[i, p])))
+    for load, _ in todo:
+        load.start()
+    for load, store in todo:
+        load.wait()
+        store.start()
+    for _, store in todo:
+        store.wait()
 
 
 def solution(mesh):
@@ -408,7 +435,14 @@
             ],
             compiler_params=pltpu.CompilerParams(collective_id=0, has_side_effects=True, vmem_limit_bytes=67043328),
         )(x, dy, w_gate, w_up, w_down)
-        return outs[:3]
+        shapes = [jax.ShapeDtypeStruct(o.shape, bf16) for o in outs[:3]]
+        return pl.pallas_call(
+            settle,
+            out_shape=shapes,
+            in_specs=[hbm] * 3,
+            out_specs=[hbm] * 3,
+            scratch_shapes=[vmem(o.shape[1:], bf16) for o in shapes] + [dma((3, 2)), dma((3, 2))],
+        )(*outs[:3])
 
     return jax.shard_map(
         step,

time: 228 us -> 218 us (0.956)
  local copies, waits for them, and re-layouts: 5.89 us -> 0 us
  Pallas kernels: 221 us -> 217 us
    pallas_call x1, Pallas kernels: 221 us -> 213 us  [step(): pl.pallas_call(functools.partial(kernel, stages), out_shape=(jax.ShapeDty...]
    unnamed x7 -> x0, local copies, waits for them, and re-layouts: 5.89 us -> none
    pallas_call x0 -> x1, Pallas kernels: none -> 3.97 us  [step(): pl.pallas_call(settle, out_shape=shapes, in_specs=[hbm] * 3, out_specs=[h...]
where the time goes in v4:
time: 218 us
  Pallas kernels  217 us (100%)
    pallas_call x1, Pallas kernels, step(): pl.pallas_call(functools.partial(kernel, stages), out_shape=(jax.ShapeDty...  213 us

profile of v4, /device:TPU:0, one launch (start us, length us, event | category | flops | bytes accessed | tf_op | source)
XLA Modules:
  0.0 217.8 jit_solution(12624339638653723381)
XLA Ops:
  0.6 213.2 %shard_map.76 = (bf16[1,512,1536]{2,1,0:T(8,128)(2,1)}, bf16[1,512,1536]{2,1,0:T(8,128)(2,1)}, bf16[1,1536,512]{2,1,0:T(8,128)(2,1)}, f32[16,512,1536]{2,1,0:T(8...) custom-call(bf16[16,512,512]{2,1,0:T(8,128)(2,1)} %x.1, ...), custom_call_target="tpu_custom_call" | custom-call | tf_op jit(solution)/shard_map/pallas_call | solution.py:413
  213.9 4.0 %shard_map.77 = (bf16[1,512,1536]{2,1,0:T(8,128)(2,1)}, bf16[1,512,1536]{2,1,0:T(8,128)(2,1)}, bf16[1,1536,512]{2,1,0:T(8,128)(2,1)}) custom-call(bf16[1,512,1536]{2,1,0:T(8,128)(2,1)} %get-tuple-element.6.a, bf16[1,512,1536]{2,1,0:T(8,128)(2,1)} %get-tuple-element.7.b, bf16[1,1536,512]{2,1,0:T(8,128)(2,1)} %get-tuple-element.8.c), custom_call_target="tpu_custom_call" | custom-call | tf_op jit(solution)/shard_map/pallas_call | solution.py:439

commit v5 on v4

--- a/solution.py
+++ b/solution.py
@@ -12,20 +12,20 @@
 OUTS = 3
 PIECES = 2
 FINE = 4
-EARLY, LATE = 3, 3
+EARLY, LATE = 4, 4
 TURN_H, VIA_H, TURN_G, VIA_G = 3, 0, 4, 7
-CODES_H = (8, 9, 10, 11, 13, 17, 18, 20, 21, 23, 24, 25, 28, 30, 31)
-CODES_G = (0, 3, 5, 6, 10, 14, 15, 17)
-LENGTHS = [107, 92, 92, 92, 92, 92, 92, 100]
+CODES_H = (8, 10, 11, 12, 14, 16, 17, 18, 19, 21, 22, 23, 25, 26, 27, 29, 31)
+CODES_G = (0, 1, 5, 8, 13, 17)
+LENGTHS = [113, 96, 96, 96, 96, 96, 96, 102]
 TABLE = (
-    (0, 0, 98621439, 31327724, 395730523, 426088030, 362112345, 9),
-    (0, 0, 307270693, 426083428, 426088025, 362112345, 9, 0),
-    (0, 100990976, 140001668, 102110341, 426088025, 362112345, 9, 0),
-    (0, 274808832, 369435654, 293962080, 426088006, 362112345, 9, 0),
-    (268435456, 92291460, 23091288, 5788248, 307779606, 362112345, 9, 0),
-    (335544320, 541139992, 404100613, 101815812, 370541956, 362112326, 9, 0),
-    (537198592, 38806917, 542246277, 139986309, 542639493, 361060437, 9, 0),
-    (23069952, 940892512, 87610405, 344318034, 561125296, 369448980, 611461, 0),
+    (0, 0, 125828144, 813052280, 912160662, 630610777, 374707557, 38245),
+    (0, 0, 26240256, 374956313, 374957462, 358963542, 2390, 0),
+    (0, 557842432, 610341009, 555238932, 374957457, 358963542, 2390, 0),
+    (0, 407109632, 152584484, 105156997, 374957156, 358963542, 2390, 0),
+    (0, 100734996, 76842369, 345375073, 92561688, 358963542, 2390, 0),
+    (0, 68293012, 610361366, 629168145, 542708292, 358963285, 2390, 0),
+    (537198592, 21585925, 92364882, 86005848, 360732760, 357045601, 2390, 0),
+    (23069952, 629345632, 369576016, 815040352, 567809157, 139821396, 9789525, 0),
 )
 TILE = 256
 
@@ -173,6 +173,7 @@
         o = lax.rem(m, OUTS)
         remote(h_out.at[o], h_v.at[m], hs_sem.at[o], h_sem.at[m, 0], me + 1).wait_send()
 
+    outs = [pltpu.make_async_copy(b, a.at[0], o_sem.at[i]) for i, (a, b) in enumerate(((og, wg), (ou, wu), (od, wd)))]
     saved = ((si_v, si_h), (m_v, m_h), (hid_v, hid_h))
 
     def spill_out(m, p, at):
@@ -298,9 +299,20 @@
 
     def do_weights(m):
         slot = jnp.where(spill, 1 + lax.rem(m, 2), lax.rem(m, SLOTS))
-        weights_term(acc_g, at_v, dg_v)
-        weights_term(acc_u, at_v, du_v)
-        weights_term(acc_d, gt_v, hid_v.at[slot])
+        terms = (acc_g, at_v, dg_v), (acc_u, at_v, du_v), (acc_d, gt_v, hid_v.at[slot])
+
+        @pl.when(m < micro - 1)
+        def _():
+            for term in terms:
+                weights_term(*term)
+
+        @pl.when(m == micro - 1)
+        def _():
+            for i, (term, w, out) in enumerate(zip(terms, (wg, wu, wd), outs, strict=True)):
+                weights_term(*term)
+                total = term[0][...].astype(bf16)
+                w[...] = total.T if i == 2 else total
+                out.start()
 
     def do_relay(n):
         def hop(codes, dst, recv, to):
@@ -358,14 +370,6 @@
         return lax.fori_loop(0, jnp.minimum(15, total - 15 * w), turn, (word, *carry))[1:]
 
     lax.fori_loop(0, lax.div(total + 14, 15), block, (jnp.int32(0),) * 5)
-
-    wg[...] = acc_g[...].astype(bf16)
-    outs = [pltpu.make_async_copy(b, a.at[0], o_sem.at[i]) for i, (a, b) in enumerate(((og, wg), (ou, wu), (od, wd)))]
-    outs[0].start()
-    wu[...] = acc_u[...].astype(bf16)
-    outs[1].start()
-    wd[...] = acc_d[...].astype(bf16).T
-    outs[2].start()
 
     @pl.when(me < stages - 1)
     def _():

time: 218 us -> 214 us (0.982)
  Pallas kernels: 217 us -> 213 us
    pallas_call x1, Pallas kernels: 213 us -> 209 us  [step(): pl.pallas_call(functools.partial(kernel, stages), out_shape=(jax.ShapeDty...]
where the time goes in v5:
time: 214 us
  Pallas kernels  213 us (100%)
    pallas_call x1, Pallas kernels, step(): pl.pallas_call(functools.partial(kernel, stages), out_shape=(jax.ShapeDty...  209 us

profile of v5, /device:TPU:0, one launch (start us, length us, event | category | flops | bytes accessed | tf_op | source)
XLA Modules:
  0.0 213.9 jit_solution(13156450616161894019)
XLA Ops:
  0.6 209.3 %shard_map.76 = (bf16[1,512,1536]{2,1,0:T(8,128)(2,1)}, bf16[1,512,1536]{2,1,0:T(8,128)(2,1)}, bf16[1,1536,512]{2,1,0:T(8,128)(2,1)}, f32[16,512,1536]{2,1,0:T(8...) custom-call(bf16[16,512,512]{2,1,0:T(8,128)(2,1)} %x.1, ...), custom_call_target="tpu_custom_call" | custom-call | tf_op jit(solution)/shard_map/pallas_call | solution.py:417
  209.9 4.0 %shard_map.77 = (bf16[1,512,1536]{2,1,0:T(8,128)(2,1)}, bf16[1,512,1536]{2,1,0:T(8,128)(2,1)}, bf16[1,1536,512]{2,1,0:T(8,128)(2,1)}) custom-call(bf16[1,512,1536]{2,1,0:T(8,128)(2,1)} %get-tuple-element.6.a, bf16[1,512,1536]{2,1,0:T(8,128)(2,1)} %get-tuple-element.7.b, bf16[1,1536,512]{2,1,0:T(8,128)(2,1)} %get-tuple-element.8.c), custom_call_target="tpu_custom_call" | custom-call | tf_op jit(solution)/shard_map/pallas_call | solution.py:443

commit v6 on v5

--- a/solution.py
+++ b/solution.py
@@ -115,15 +115,6 @@
     for load in loads:
         load.start()
 
-    @pl.when(first)
-    def _():
-        for m in range(1, EARLY):
-            load_pieces(m, x, h_v, h_sem, FINE)
-
-        @pl.loop(EARLY, micro)
-        def _(m):
-            load_pieces(m, x, h_v, h_sem)
-
     @pl.when(last)
     def _():
         @pl.loop(0, micro - LATE)
@@ -139,7 +130,16 @@
         load.wait()
     pl.semaphore_wait(barrier, stages - 1)
 
-    @pl.when(me > 0)
+    @pl.when(first)
+    def _():
+        for m in range(1, EARLY):
+            load_pieces(m, x, h_v, h_sem, FINE)
+
+        @pl.loop(EARLY, micro)
+        def _(m):
+            load_pieces(m, x, h_v, h_sem)
+
+    @pl.when(me > 1)
     def _():
         wgt[...] = wg[...].T
         wut[...] = wu[...].T
@@ -255,8 +255,10 @@
         p = jnp.where(fine, lax.rem(late, FINE), lax.rem(n, PIECES))
         slot = jnp.where(spill, 1 + lax.rem(m, 2), lax.rem(m, SLOTS))
 
-        @pl.when(first & (n == 0))
-        def _():
+        @pl.when((me <= 1) & (n == 0))
+        def _():
+            wgt[...] = wg[...].T
+            wut[...] = wu[...].T
             wdt[...] = wd[...].T
 
         @pl.when(spill & (p == 0))

time: 214 us -> 214 us (level)
  no operation moved by 1% of the time
where the time goes in v6:
time: 214 us
  Pallas kernels  213 us (100%)
    pallas_call x1, Pallas kernels, step(): pl.pallas_call(functools.partial(kernel, stages), out_shape=(jax.ShapeDty...  209 us

profile of v6, /device:TPU:0, one launch (start us, length us, event | category | flops | bytes accessed | tf_op | source)
XLA Modules:
  0.0 214.1 jit_solution(18021835638441357322)
XLA Ops:
  0.6 209.4 %shard_map.76 = (bf16[1,512,1536]{2,1,0:T(8,128)(2,1)}, bf16[1,512,1536]{2,1,0:T(8,128)(2,1)}, bf16[1,1536,512]{2,1,0:T(8,128)(2,1)}, f32[16,512,1536]{2,1,0:T(8...) custom-call(bf16[16,512,512]{2,1,0:T(8,128)(2,1)} %x.1, ...), custom_call_target="tpu_custom_call" | custom-call | tf_op jit(solution)/shard_map/pallas_call | solution.py:419
  210.1 4.0 %shard_map.77 = (bf16[1,512,1536]{2,1,0:T(8,128)(2,1)}, bf16[1,512,1536]{2,1,0:T(8,128)(2,1)}, bf16[1,1536,512]{2,1,0:T(8,128)(2,1)}) custom-call(bf16[1,512,1536]{2,1,0:T(8,128)(2,1)} %get-tuple-element.6.a, bf16[1,512,1536]{2,1,0:T(8,128)(2,1)} %get-tuple-element.7.b, bf16[1,1536,512]{2,1,0:T(8,128)(2,1)} %get-tuple-element.8.c), custom_call_target="tpu_custom_call" | custom-call | tf_op jit(solution)/shard_map/pallas_call | solution.py:445
